TPU v7x, 32 devices: a whole 2x2x4 slice. The times are simulated.
32 devices in a mesh: gx: 8 (over z, x), gz: 4 (over y, core).
Axes of the slice: x: 2, y: 2, z: 4, core: 2. Of those that a mesh axis runs over, the one named last changes fastest.
Arguments:
- velocity: float32 [3, 64, 128, 384], P(None, 'gx', 'gz'), may hold values from -6 to 6
- y_gap: float32 [385], replicated, may hold values from 0.2 to 2
Outputs:
- eddy_visc: float32 [64, 128, 384], P('gx', 'gz')
- lm_field: float32 [64, 128, 384], P('gx', 'gz')
- mm_field: float32 [64, 128, 384], P('gx', 'gz')
- coefficient: float32 [384], replicated
All inputs are finite; a program needn't handle non-finite values.
Results may differ from a plain program's by a relative error of at most 0.00002.
Values sent between devices are 32-bit elements; how exact they have to be, the bound alone decides.
A program may use at most 64 MiB of HBM per device.

v0:
```python
import jax
import jax.numpy as jnp
from jax import lax
from jax.sharding import PartitionSpec as P

WEIGHTS = (1.0, 1.0, 1.0, 2.0, 2.0, 2.0)


def extended(array, sides, width):
    for axis, dim in sides:
        size, length = (lax.axis_size(axis), array.shape[dim])
        up = [(i, (i + 1) % size) for i in range(size)]
        down = [(j, i) for i, j in up]
        last = lax.slice_in_dim(array, length - width, length, axis=dim)
        leading = lax.slice_in_dim(array, 0, width, axis=dim)
        before = lax.ppermute(last, axis, up)
        after = lax.ppermute(leading, axis, down)
        array = jnp.concatenate([before, array, after], axis=dim)
    return array


def wall_slope(values, y_gap):
    padded = jnp.pad(values, [(0, 0)] * (values.ndim - 1) + [(1, 1)])
    return (padded[..., 2:] - padded[..., :-2]) / (y_gap[:-1] + y_gap[1:])


def strain_parts(slope_x, slope_y, slope_z):
    return jnp.stack(
        [
            slope_x[0],
            slope_y[1],
            slope_z[2],
            0.5 * (slope_y[0] + slope_x[1]),
            0.5 * (slope_z[0] + slope_x[2]),
            0.5 * (slope_z[1] + slope_y[2]),
        ]
    )


def contract(first_part, second_part):
    summed = first_part[0] * second_part[0]
    for component in range(1, 6):
        summed = summed + WEIGHTS[component] * first_part[component] * second_part[component]
    return summed


def magnitude(strain):
    return jnp.sqrt(2.0 * contract(strain, strain))


def pair_products(speeds):
    return jnp.stack(
        [
            speeds[0] * speeds[0],
            speeds[1] * speeds[1],
            speeds[2] * speeds[2],
            speeds[0] * speeds[1],
            speeds[0] * speeds[2],
            speeds[1] * speeds[2],
        ]
    )


def width_square(y_gap):
    return (0.5 * (y_gap[:-1] + y_gap[1:])) ** (2.0 / 3.0)


def germano(smooth_velocity, smooth_pairs, smooth_stress, test_strain, width_sq):
    leonard = smooth_pairs - pair_products(smooth_velocity)
    model_term = 2.0 * width_sq * (smooth_stress - 4.0 * magnitude(test_strain) * test_strain)
    return (contract(leonard, model_term), contract(model_term, model_term))


def rim_strain(padded, y_gap):
    slope_x = (padded[:, 2:, 1:-1] - padded[:, :-2, 1:-1]) * 0.5
    slope_z = (padded[:, 1:-1, 2:] - padded[:, 1:-1, :-2]) * 0.5
    slope_y = wall_slope(padded[:, 1:-1, 1:-1], y_gap)
    return strain_parts(slope_x, slope_y, slope_z)


def rim_filter(values):
    along_x = 0.25 * values[:, :-2] + 0.5 * values[:, 1:-1] + 0.25 * values[:, 2:]
    return 0.25 * along_x[:, :, :-2] + 0.5 * along_x[:, :, 1:-1] + 0.25 * along_x[:, :, 2:]


def per_device(velocity, y_gap):
    width_sq = width_square(y_gap)
    padded = extended(velocity, (("gx", 1), ("gz", 2)), 2)
    strain_wide = rim_strain(padded, y_gap)
    size_wide = magnitude(strain_wide)
    inner = padded[:, 1:-1, 1:-1]
    smooth_pairs = rim_filter(pair_products(inner))
    smooth_stress = rim_filter(size_wide * strain_wide)
    smooth_wide = rim_filter(padded)
    smooth_velocity = smooth_wide[:, 1:-1, 1:-1]
    test_strain = rim_strain(smooth_wide, y_gap)
    strain_size = size_wide[1:-1, 1:-1]
    lm_field, mm_field = germano(
        smooth_velocity, smooth_pairs, smooth_stress, test_strain, width_sq
    )
    planes = velocity.shape[1] * lax.axis_size("gx") * velocity.shape[2] * lax.axis_size("gz")
    plane_pair = jnp.stack([jnp.sum(lm_field, axis=(0, 1)), jnp.sum(mm_field, axis=(0, 1))])
    total_pair = lax.psum(plane_pair, ("gx", "gz"))
    coefficient = total_pair[0] / planes / (total_pair[1] / planes + 1e-06)
    eddy_visc = coefficient * width_sq * strain_size
    return (eddy_visc, lm_field, mm_field, coefficient)


def solution(mesh):
    placed = (P(None, "gx", "gz", None), P())
    return jax.shard_map(
        per_device,
        mesh=mesh,
        in_specs=placed,
        out_specs=(P("gx", "gz", None), P("gx", "gz", None), P("gx", "gz", None), P()),
        check_vma=False,
    )
```

profile of v0, /device:TPU:0, one launch (start us, length us, event | category | flops | bytes accessed | tf_op | source)
XLA Modules:
  0.0 76.4 jit_solution(4850961541052591493)
XLA Ops:
  0.7 1.2 %fusion.70 = (f32[3,2,32,384]{3,2,1,0:T(8,128)S(1)}, f32[3,2,32,384]{3,2,1,0:T(8,128)S(1)}) fusion(f32[3,8,32,384]{3,2,1,0:T(8,128)} %param.2), kind=kLoop, calls=%fused_computation.159 | loop fusion | bytes 1179648 | tf_op jit(solution)/shard_map/slice | solution.py:15
  1.8 3.0 %collective-permute-start = (f32[3,2,32,384]{3,2,1,0:T(8,128)S(1)}, f32[3,2,32,384]{3,2,1,0:T(8,128)S(1)}, u32[]{:S(2)}, u32[]{:S(2)}) collective-permute-start(f32[3,2,32,384]{3,2,1,0:T(8,128)S(1)} %get-tuple-element.30), channel_id=1, source_target_pairs={{0,4},{4,8},{8,12},{12,16},{16,20},{20,24},{24,28},{28,0},{1,5},{5... | collective-permute-start | bytes 884744 | tf_op jit(solution)/shard_map/ppermute | solution.py:16
  4.9 3.1 %collective-permute-start.1 = (f32[3,2,32,384]{3,2,1,0:T(8,128)S(1)}, f32[3,2,32,384]{3,2,1,0:T(8,128)S(1)}, u32[]{:S(2)}, u32[]{:S(2)}) collective-permute-start(f32[3,2,32,384]{3,2,1,0:T(8,128)S(1)} %get-tuple-element.29), channel_id=1, source_target_pairs={{4,0},{8,4},{12,8},{16,12},{20,16},{24,20},{28,24},{0,28},{5,1},{9... | collective-permute-start | bytes 884744 | tf_op jit(solution)/shard_map/ppermute | solution.py:17
  8.0 9.5 %collective-permute-done = f32[3,2,32,384]{3,2,1,0:T(8,128)S(1)} collective-permute-done((f32[3,2,32,384]{3,2,1,0:T(8,128)S(1)}, f32[3,2,32,384]{3,2,1,0:T(8,128)S(1)}, u32[]{:S(2)}, u32[]{:S(2)}) %collective-permute-start) | collective-permute-done | bytes 294944 | tf_op jit(solution)/shard_map/ppermute | solution.py:16
  17.5 0.1 constant_dynamic-update-slice_fusion.1
  17.6 2.1 %collective-permute-done.1 = f32[3,2,32,384]{3,2,1,0:T(8,128)S(1)} collective-permute-done((f32[3,2,32,384]{3,2,1,0:T(8,128)S(1)}, f32[3,2,32,384]{3,2,1,0:T(8,128)S(1)}, u32[]{:S(2)}, u32[]{:S(2)}) %collective-permute-start.1) | collective-permute-done | bytes 294944 | tf_op jit(solution)/shard_map/ppermute | solution.py:17
  19.8 0.5 collective-permute-start.2
  20.3 0.1 fusion.58
  20.4 1.8 %collective-permute-done.3 = f32[3,12,2,384]{3,2,1,0:T(2,128)S(1)} collective-permute-done((f32[3,12,2,384]{3,2,1,0:T(2,128)S(1)}, f32[3,12,2,384]{3,2,1,0:T(2,128)S(1)}, u32[]{:S(2)}, u32[]{:S(2)}) %collective-permute-start.3) | collective-permute-done | bytes 110624 | tf_op jit(solution)/shard_map/ppermute | solution.py:17
  22.3 3.0 %collective-permute-done.2 = f32[3,12,2,384]{3,2,1,0:T(2,128)S(1)} collective-permute-done((f32[3,12,2,384]{3,2,1,0:T(2,128)S(1)}, f32[3,12,2,384]{3,2,1,0:T(2,128)S(1)}, u32[]{:S(2)}, u32[]{:S(2)}) %collective-permute-start.2) | collective-permute-done | bytes 110624 | tf_op jit(solution)/shard_map/ppermute | solution.py:16
  25.2 0.3 pad_maximum_fusion
  25.5 0.3 fusion.15
  25.8 0.3 fusion.18
  26.0 0.5 fusion.16
  26.6 0.4 fusion.22
  27.1 1.3 %fusion.12 = (f32[3,10,34,384]{3,2,1,0:T(8,128)S(1)}, f32[3,10,34,384]{3,2,1,0:T(8,128)S(1)}) fusion(f32[3,10,34,384]{3,2,1,0:T(8,128)S(1)} %get-tuple-element.22, f32[384]{0:T(512)S(1)} %get-tuple-element.9, f32[3,12,32,384]{3,2,1,0:T(8,128)S(1)} %constant_dynamic-update-slice_fusion, f32[3,12,2,384]{3,2,1,0:T(2,128)S(1)} %collective-permute-done.2, ...), kind=kLoop, calls=%fused_computation.27 | loop fusion | flops 2350080 | bytes 6692352 | tf_op jit(solution)/shard_map/div | solution.py:24
  28.5 0.6 fusion.29
  29.2 0.1 multiply_dynamic-update-slice_fusion.1
  29.3 0.1 multiply_dynamic-update-slice_fusion
  29.4 0.3 broadcast_multiply_fusion
  29.6 0.4 fusion
  30.1 0.7 fusion.21
  30.8 0.4 fusion.36
  31.8 0.1 multiply_dynamic-update-slice_fusion.5
  31.9 0.1 multiply_dynamic-update-slice_fusion.4
  32.0 0.1 multiply_dynamic-update-slice_fusion.3
  32.2 0.4 fusion.2
  32.6 0.9 %fusion.9 = f32[6,8,32,384]{3,2,1,0:T(8,128)S(1)} fusion(f32[6,8,32,384]{3,2,1,0:T(8,128)S(1)} %multiply_dynamic-update-slice_fusion.12, f32[6,8,34,384]{3,2,1,0:T(8,128)S(1)} %fusion.2), kind=kLoop, calls=%fused_computation.21 | loop fusion | flops 3538944 | bytes 11796480 | tf_op jit(solution)/shard_map/sub | solution.py:69
  33.5 0.9 %fusion.6 = f32[6,8,32,384]{3,2,1,0:T(8,128)S(1)} fusion(f32[6,8,34,384]{3,2,1,0:T(8,128)S(1)} %fusion, f32[6,8,32,384]{3,2,1,0:T(8,128)S(1)} %multiply_dynamic-update-slice_fusion.9, f32[8,32,384]{2,1,0:T(8,128)S(1)} %get-tuple-element.19, f32[384]{0:T(512)S(1)} %get-tuple-element.8), kind=kLoop, calls=%fused_computation.15 | loop fusion | flops 4718592 | bytes 12191232 | tf_op jit(solution)/shard_map/mul | solution.py:70
  34.4 1.4 %fusion.65 = (f32[384]{0:T(512)S(1)}, f32[8,32,384]{2,1,0:T(8,128)}, f32[384]{0:T(512)S(1)}, f32[8,32,384]{2,1,0:T(8,128)}) fusion(f32[6,8,32,384]{3,2,1,0:T(8,128)S(1)} %fusion.6, f32[6,8,32,384]{3,2,1,0:T(8,128)S(1)} %fusion.9), kind=kLoop, calls=%fused_computation.156 | loop fusion | flops 2948352 | bytes 5508096 | tf_op jit(solution)/shard_map/reduce_sum | solution.py:102
  35.8 39.4 %psum.7 = f32[2,384]{1,0:T(2,128)S(1)} all-reduce(f32[2,384]{1,0:T(2,128)S(1)} %pad_maximum_fusion.3), channel_id=1, replica_groups=mesh['gx'=8,'gz'=4] {'gx','gz'}, use_global_device_ids=true, to_apply=%region_2.3 | all-reduce | flops 768 | bytes 6144 | tf_op jit(solution)/shard_map/psum | solution.py:103
  75.2 1.1 %fusion.44 = f32[8,32,384]{2,1,0:T(8,128)} fusion(f32[10,34,384]{2,1,0:T(8,128)S(1)} %get-tuple-element.14, f32[10,34,384]{2,1,0:T(8,128)S(1)} %get-tuple-element.12, f32[10,34,384]{2,1,0:T(8,128)S(1)} %get-tuple-element.16, f32[10,34,384]{2,1,0:T(8,128)S(1)} %broadcast_multiply_fusion.1, f32[10,34,384]{2,1,0:T(8,128)S(1)} %bitcast.69, f32[384]{0:T(512)S(1)} %fusion.57), kind=kLoop, calls=%fused_computation.103 | loop fusion | flops 983040 | bytes 2360832 | tf_op jit(solution)/shard_map/mul | solution.py:105
  (33 shorter events, 1.1 us)
Async XLA Ops:
  0.6 16.8 %copy-start = (f32[3,8,32,384]{3,2,1,0:T(8,128)S(1)}, f32[3,8,32,384]{3,2,1,0:T(8,128)}, u32[]{:S(2)}) copy-start(f32[3,8,32,384]{3,2,1,0:T(8,128)} %param.2) | copy-start | bytes 3538948
  0.6 19.7 %copy-start.2 = (f32[385]{0:T(512)S(1)}, f32[385]{0:T(512)}, u32[]{:S(2)}) copy-start(f32[385]{0:T(512)} %param.3) | copy-start | bytes 4624
  1.8 15.6 %collective-permute-start = (f32[3,2,32,384]{3,2,1,0:T(8,128)S(1)}, f32[3,2,32,384]{3,2,1,0:T(8,128)S(1)}, u32[]{:S(2)}, u32[]{:S(2)}) collective-permute-start(f32[3,2,32,384]{3,2,1,0:T(8,128)S(1)} %get-tuple-element.30), channel_id=1, source_target_pairs={{0,4},{4,8},{8,12},{12,16},{16,20},{20,24},{24,28},{28,0},{1,5},{5... | collective-permute-start | bytes 884744 | tf_op jit(solution)/shard_map/ppermute | solution.py:16
  4.9 14.8 %collective-permute-start.1 = (f32[3,2,32,384]{3,2,1,0:T(8,128)S(1)}, f32[3,2,32,384]{3,2,1,0:T(8,128)S(1)}, u32[]{:S(2)}, u32[]{:S(2)}) collective-permute-start(f32[3,2,32,384]{3,2,1,0:T(8,128)S(1)} %get-tuple-element.29), channel_id=1, source_target_pairs={{4,0},{8,4},{12,8},{16,12},{20,16},{24,20},{28,24},{0,28},{5,1},{9... | collective-permute-start | bytes 884744 | tf_op jit(solution)/shard_map/ppermute | solution.py:17
  19.8 2.5 %collective-permute-start.3 = (f32[3,12,2,384]{3,2,1,0:T(2,128)S(1)}, f32[3,12,2,384]{3,2,1,0:T(2,128)S(1)}, u32[]{:S(2)}, u32[]{:S(2)}) collective-permute-start(f32[3,12,2,384]{3,2,1,0:T(2,128)S(1)} %get-tuple-element.28), channel_id=1, source_target_pairs={{1,0},{2,1},{3,2},{0,3},{5,4},{6,5},{7,6},{4,7},{9,8},{10,9},{11,1... | collective-permute-start | bytes 331784 | tf_op jit(solution)/shard_map/ppermute | solution.py:17
  19.8 5.4 %collective-permute-start.2 = (f32[3,12,2,384]{3,2,1,0:T(2,128)S(1)}, f32[3,12,2,384]{3,2,1,0:T(2,128)S(1)}, u32[]{:S(2)}, u32[]{:S(2)}) collective-permute-start(f32[3,12,2,384]{3,2,1,0:T(2,128)S(1)} %get-tuple-element.27), channel_id=1, source_target_pairs={{0,1},{1,2},{2,3},{3,0},{4,5},{5,6},{6,7},{7,4},{8,9},{9,10},{10,1... | collective-permute-start | bytes 331784 | tf_op jit(solution)/shard_map/ppermute | solution.py:16
  75.2 1.2 %copy-start.1 = (f32[384]{0:T(512)}, f32[384]{0:T(512)S(1)}, u32[]{:S(2)}) copy-start(f32[384]{0:T(512)S(1)} %fusion.61) | copy-start | bytes 4612
where the time goes:
time: 76.6 us; the launch traced here: 76.4 us
  blocking collectives  39.4 us (51%)
  waiting for transfers between devices  16.4 us (21%)
  other arithmetic  11.4 us (15%)
  starting transfers between devices  6.68 us (9%)
  local copies, waits for them, and re-layouts  1.59 us (2%)
  between operations  0.97 us (1%)
    psum x1, blocking collectives, per_device(): total_pair = lax.psum(plane_pair, ('gx', 'gz'))  39.4 us
    ppermute x2, waiting for transfers between devices, extended(): before = lax.ppermute(last, axis, up)  12.4 us
    ppermute x2, waiting for transfers between devices, extended(): after = lax.ppermute(leading, axis, down)  3.91 us
    ppermute x2, starting transfers between devices, extended(): before = lax.ppermute(last, axis, up)  3.52 us
    ppermute x2, starting transfers between devices, extended(): after = lax.ppermute(leading, axis, down)  3.16 us
    div x2, other arithmetic, wall_slope(): return (padded[..., 2:] - padded[..., :-2]) / (y_gap[:-1] + y_gap[1:])  1.94 us
  transfers between devices with their start and end apart: 4, of which 4 were waited for; matrix products, arithmetic and copies ran while one was open for 0% of the time, Pallas kernels for 0%

commit v1 on v0

--- a/solution.py
+++ b/solution.py
@@ -100,7 +100,7 @@
     )
     planes = velocity.shape[1] * lax.axis_size("gx") * velocity.shape[2] * lax.axis_size("gz")
     plane_pair = jnp.stack([jnp.sum(lm_field, axis=(0, 1)), jnp.sum(mm_field, axis=(0, 1))])
-    total_pair = lax.psum(plane_pair, ("gx", "gz"))
+    total_pair = jnp.sum(lax.all_gather(plane_pair, ("gx", "gz")), axis=0)
     coefficient = total_pair[0] / planes / (total_pair[1] / planes + 1e-06)
     eddy_visc = coefficient * width_sq * strain_size
     return (eddy_visc, lm_field, mm_field, coefficient)

time: 76.6 us -> 77.3 us (level)
    all_gather x0 -> x1, blocking collectives: none -> 40.1 us  [per_device(): total_pair = jnp.sum(lax.all_gather(plane_pair, ('gx', 'gz')), axis=0)]
    psum x1 -> x0, blocking collectives: 39.4 us -> none  [per_device(): total_pair = lax.psum(plane_pair, ('gx', 'gz'))]
where the time goes in v1:
time: 77.3 us; the launch traced here: 77.1 us
  blocking collectives  40.1 us (52%)
  waiting for transfers between devices  16.4 us (21%)
  other arithmetic  11.5 us (15%)
  starting transfers between devices  6.68 us (9%)
  local copies, waits for them, and re-layouts  1.59 us (2%)
  between operations  0.96 us (1%)
    all_gather x1, blocking collectives, per_device(): total_pair = jnp.sum(lax.all_gather(plane_pair, ('gx', 'gz')), axis=0)  40.1 us
    ppermute x2, waiting for transfers between devices, extended(): before = lax.ppermute(last, axis, up)  12.4 us
    ppermute x2, waiting for transfers between devices, extended(): after = lax.ppermute(leading, axis, down)  3.91 us
    ppermute x2, starting transfers between devices, extended(): before = lax.ppermute(last, axis, up)  3.52 us
    ppermute x2, starting transfers between devices, extended(): after = lax.ppermute(leading, axis, down)  3.16 us
    div x2, other arithmetic, wall_slope(): return (padded[..., 2:] - padded[..., :-2]) / (y_gap[:-1] + y_gap[1:])  1.94 us
  transfers between devices with their start and end apart: 4, of which 4 were waited for; matrix products, arithmetic and copies ran while one was open for 0% of the time, Pallas kernels for 0%

profile of v1, /device:TPU:0, one launch (start us, length us, event | category | flops | bytes accessed | tf_op | source)
XLA Modules:
  0.0 77.1 jit_solution(4728190419374331492)
XLA Ops:
  0.7 1.2 %fusion.70 = (f32[3,2,32,384]{3,2,1,0:T(8,128)S(1)}, f32[3,2,32,384]{3,2,1,0:T(8,128)S(1)}) fusion(f32[3,8,32,384]{3,2,1,0:T(8,128)} %param.2), kind=kLoop, calls=%fused_computation.159 | loop fusion | bytes 1179648 | tf_op jit(solution)/shard_map/slice | solution.py:15
  1.8 3.0 %collective-permute-start = (f32[3,2,32,384]{3,2,1,0:T(8,128)S(1)}, f32[3,2,32,384]{3,2,1,0:T(8,128)S(1)}, u32[]{:S(2)}, u32[]{:S(2)}) collective-permute-start(f32[3,2,32,384]{3,2,1,0:T(8,128)S(1)} %get-tuple-element.30), channel_id=1, source_target_pairs={{0,4},{4,8},{8,12},{12,16},{16,20},{20,24},{24,28},{28,0},{1,5},{5... | collective-permute-start | bytes 884744 | tf_op jit(solution)/shard_map/ppermute | solution.py:16
  4.9 3.1 %collective-permute-start.1 = (f32[3,2,32,384]{3,2,1,0:T(8,128)S(1)}, f32[3,2,32,384]{3,2,1,0:T(8,128)S(1)}, u32[]{:S(2)}, u32[]{:S(2)}) collective-permute-start(f32[3,2,32,384]{3,2,1,0:T(8,128)S(1)} %get-tuple-element.29), channel_id=1, source_target_pairs={{4,0},{8,4},{12,8},{16,12},{20,16},{24,20},{28,24},{0,28},{5,1},{9... | collective-permute-start | bytes 884744 | tf_op jit(solution)/shard_map/ppermute | solution.py:17
  8.0 9.5 %collective-permute-done = f32[3,2,32,384]{3,2,1,0:T(8,128)S(1)} collective-permute-done((f32[3,2,32,384]{3,2,1,0:T(8,128)S(1)}, f32[3,2,32,384]{3,2,1,0:T(8,128)S(1)}, u32[]{:S(2)}, u32[]{:S(2)}) %collective-permute-start) | collective-permute-done | bytes 294944 | tf_op jit(solution)/shard_map/ppermute | solution.py:16
  17.5 0.1 constant_dynamic-update-slice_fusion.1
  17.6 2.1 %collective-permute-done.1 = f32[3,2,32,384]{3,2,1,0:T(8,128)S(1)} collective-permute-done((f32[3,2,32,384]{3,2,1,0:T(8,128)S(1)}, f32[3,2,32,384]{3,2,1,0:T(8,128)S(1)}, u32[]{:S(2)}, u32[]{:S(2)}) %collective-permute-start.1) | collective-permute-done | bytes 294944 | tf_op jit(solution)/shard_map/ppermute | solution.py:17
  19.8 0.5 collective-permute-start.2
  20.3 0.1 fusion.58
  20.4 1.8 %collective-permute-done.3 = f32[3,12,2,384]{3,2,1,0:T(2,128)S(1)} collective-permute-done((f32[3,12,2,384]{3,2,1,0:T(2,128)S(1)}, f32[3,12,2,384]{3,2,1,0:T(2,128)S(1)}, u32[]{:S(2)}, u32[]{:S(2)}) %collective-permute-start.3) | collective-permute-done | bytes 110624 | tf_op jit(solution)/shard_map/ppermute | solution.py:17
  22.3 3.0 %collective-permute-done.2 = f32[3,12,2,384]{3,2,1,0:T(2,128)S(1)} collective-permute-done((f32[3,12,2,384]{3,2,1,0:T(2,128)S(1)}, f32[3,12,2,384]{3,2,1,0:T(2,128)S(1)}, u32[]{:S(2)}, u32[]{:S(2)}) %collective-permute-start.2) | collective-permute-done | bytes 110624 | tf_op jit(solution)/shard_map/ppermute | solution.py:16
  25.2 0.3 pad_maximum_fusion
  25.5 0.3 fusion.15
  25.8 0.3 fusion.18
  26.0 0.5 fusion.16
  26.6 0.4 fusion.22
  27.1 1.3 %fusion.12 = (f32[3,10,34,384]{3,2,1,0:T(8,128)S(1)}, f32[3,10,34,384]{3,2,1,0:T(8,128)S(1)}) fusion(f32[3,10,34,384]{3,2,1,0:T(8,128)S(1)} %get-tuple-element.22, f32[384]{0:T(512)S(1)} %get-tuple-element.9, f32[3,12,32,384]{3,2,1,0:T(8,128)S(1)} %constant_dynamic-update-slice_fusion, f32[3,12,2,384]{3,2,1,0:T(2,128)S(1)} %collective-permute-done.2, ...), kind=kLoop, calls=%fused_computation.27 | loop fusion | flops 2350080 | bytes 6692352 | tf_op jit(solution)/shard_map/div | solution.py:24
  28.5 0.6 fusion.29
  29.2 0.1 multiply_dynamic-update-slice_fusion.1
  29.3 0.1 multiply_dynamic-update-slice_fusion
  29.4 0.3 broadcast_multiply_fusion
  29.6 0.4 fusion
  30.1 0.7 fusion.21
  30.8 0.4 fusion.36
  31.8 0.1 multiply_dynamic-update-slice_fusion.5
  31.9 0.1 multiply_dynamic-update-slice_fusion.4
  32.0 0.1 multiply_dynamic-update-slice_fusion.3
  32.2 0.4 fusion.2
  32.6 0.9 %fusion.9 = f32[6,8,32,384]{3,2,1,0:T(8,128)S(1)} fusion(f32[6,8,32,384]{3,2,1,0:T(8,128)S(1)} %multiply_dynamic-update-slice_fusion.12, f32[6,8,34,384]{3,2,1,0:T(8,128)S(1)} %fusion.2), kind=kLoop, calls=%fused_computation.21 | loop fusion | flops 3538944 | bytes 11796480 | tf_op jit(solution)/shard_map/sub | solution.py:69
  33.5 0.9 %fusion.6 = f32[6,8,32,384]{3,2,1,0:T(8,128)S(1)} fusion(f32[6,8,34,384]{3,2,1,0:T(8,128)S(1)} %fusion, f32[6,8,32,384]{3,2,1,0:T(8,128)S(1)} %multiply_dynamic-update-slice_fusion.9, f32[8,32,384]{2,1,0:T(8,128)S(1)} %get-tuple-element.19, f32[384]{0:T(512)S(1)} %get-tuple-element.8), kind=kLoop, calls=%fused_computation.15 | loop fusion | flops 4718592 | bytes 12191232 | tf_op jit(solution)/shard_map/mul | solution.py:70
  34.4 1.4 %fusion.65 = (f32[384]{0:T(512)S(1)}, f32[8,32,384]{2,1,0:T(8,128)}, f32[384]{0:T(512)S(1)}, f32[8,32,384]{2,1,0:T(8,128)}) fusion(f32[6,8,32,384]{3,2,1,0:T(8,128)S(1)} %fusion.6, f32[6,8,32,384]{3,2,1,0:T(8,128)S(1)} %fusion.9), kind=kLoop, calls=%fused_computation.156 | loop fusion | flops 2948352 | bytes 5508096 | tf_op jit(solution)/shard_map/reduce_sum | solution.py:102
  35.8 40.1 %all-gather.1 = f32[32,2,384]{2,1,0:T(2,128)S(1)} all-gather(f32[1,2,384]{2,1,0:T(2,128)S(1)} %maximum_bitcast_fusion), channel_id=2, replica_groups=mesh['gx'=8,'gz'=4] {'gx','gz'}, dimensions={0}, use_global_device_ids=true | all-gather | bytes 101376 | tf_op jit(solution)/shard_map/all_gather | solution.py:103
  76.0 1.1 %fusion.44 = f32[8,32,384]{2,1,0:T(8,128)} fusion(f32[10,34,384]{2,1,0:T(8,128)S(1)} %get-tuple-element.14, f32[10,34,384]{2,1,0:T(8,128)S(1)} %get-tuple-element.12, f32[10,34,384]{2,1,0:T(8,128)S(1)} %get-tuple-element.16, f32[10,34,384]{2,1,0:T(8,128)S(1)} %broadcast_multiply_fusion.1, f32[10,34,384]{2,1,0:T(8,128)S(1)} %bitcast.71, f32[384]{0:T(512)S(1)} %fusion.57), kind=kLoop, calls=%fused_computation.103 | loop fusion | flops 983040 | bytes 2360832 | tf_op jit(solution)/shard_map/mul | solution.py:105
  (34 shorter events, 1.2 us)
Async XLA Ops:
  0.6 16.8 %copy-start = (f32[3,8,32,384]{3,2,1,0:T(8,128)S(1)}, f32[3,8,32,384]{3,2,1,0:T(8,128)}, u32[]{:S(2)}) copy-start(f32[3,8,32,384]{3,2,1,0:T(8,128)} %param.2) | copy-start | bytes 3538948
  0.6 19.7 %copy-start.2 = (f32[385]{0:T(512)S(1)}, f32[385]{0:T(512)}, u32[]{:S(2)}) copy-start(f32[385]{0:T(512)} %param.3) | copy-start | bytes 4624
  1.8 15.6 %collective-permute-start = (f32[3,2,32,384]{3,2,1,0:T(8,128)S(1)}, f32[3,2,32,384]{3,2,1,0:T(8,128)S(1)}, u32[]{:S(2)}, u32[]{:S(2)}) collective-permute-start(f32[3,2,32,384]{3,2,1,0:T(8,128)S(1)} %get-tuple-element.30), channel_id=1, source_target_pairs={{0,4},{4,8},{8,12},{12,16},{16,20},{20,24},{24,28},{28,0},{1,5},{5... | collective-permute-start | bytes 884744 | tf_op jit(solution)/shard_map/ppermute | solution.py:16
  4.9 14.8 %collective-permute-start.1 = (f32[3,2,32,384]{3,2,1,0:T(8,128)S(1)}, f32[3,2,32,384]{3,2,1,0:T(8,128)S(1)}, u32[]{:S(2)}, u32[]{:S(2)}) collective-permute-start(f32[3,2,32,384]{3,2,1,0:T(8,128)S(1)} %get-tuple-element.29), channel_id=1, source_target_pairs={{4,0},{8,4},{12,8},{16,12},{20,16},{24,20},{28,24},{0,28},{5,1},{9... | collective-permute-start | bytes 884744 | tf_op jit(solution)/shard_map/ppermute | solution.py:17
  19.8 2.5 %collective-permute-start.3 = (f32[3,12,2,384]{3,2,1,0:T(2,128)S(1)}, f32[3,12,2,384]{3,2,1,0:T(2,128)S(1)}, u32[]{:S(2)}, u32[]{:S(2)}) collective-permute-start(f32[3,12,2,384]{3,2,1,0:T(2,128)S(1)} %get-tuple-element.28), channel_id=1, source_target_pairs={{1,0},{2,1},{3,2},{0,3},{5,4},{6,5},{7,6},{4,7},{9,8},{10,9},{11,1... | collective-permute-start | bytes 331784 | tf_op jit(solution)/shard_map/ppermute | solution.py:17
  19.8 5.4 %collective-permute-start.2 = (f32[3,12,2,384]{3,2,1,0:T(2,128)S(1)}, f32[3,12,2,384]{3,2,1,0:T(2,128)S(1)}, u32[]{:S(2)}, u32[]{:S(2)}) collective-permute-start(f32[3,12,2,384]{3,2,1,0:T(2,128)S(1)} %get-tuple-element.27), channel_id=1, source_target_pairs={{0,1},{1,2},{2,3},{3,0},{4,5},{5,6},{6,7},{7,4},{8,9},{9,10},{10,1... | collective-permute-start | bytes 331784 | tf_op jit(solution)/shard_map/ppermute | solution.py:16
  76.0 1.2 %copy-start.1 = (f32[384]{0:T(512)}, f32[384]{0:T(512)S(1)}, u32[]{:S(2)}) copy-start(f32[384]{0:T(512)S(1)} %fusion.61) | copy-start | bytes 4612
